TPU v7x, 128 devices: a whole 4x4x4 slice. The times are simulated.
128 devices in a mesh: dp: 8 (over z_lo, y), inner: 16 (over z_hi, x, core).
Axes of the slice: x: 4, y: 4, z: 4 (z_hi: 2, z_lo: 2; z = z_hi * 2 + z_lo), core: 2. Of those that a mesh axis runs over, the one named last changes fastest.
Arguments:
- queries: bfloat16 [128, 32, 128], P(('dp', 'inner'))
- labels: int32 [128], P(('dp', 'inner')), may hold values from 0 to 511
- pages: bfloat16 [512, 1024, 128], P(('dp', 'inner'))
Outputs:
- grad_queries: float32 [128, 32, 128], P(('dp', 'inner'))
- grad_pages: float32 [512, 1024, 128], P(('dp', 'inner'))
All inputs are finite; a program needn't handle non-finite values.
Results may differ from a plain program's by a relative error of at most 0.0029.
Values may be sent and summed in bfloat16 or wider, within the bound.
A program may use at most 64 MiB of HBM per device.

v0:
```python
import jax
import jax.numpy as jnp
from jax import lax
from jax.sharding import PartitionSpec as P


def in_order(pieces, dim):
    pieces = jnp.moveaxis(pieces, 0, dim)
    shape = pieces.shape
    return pieces.reshape(*shape[:dim], shape[dim] * shape[dim + 1], *shape[dim + 2 :])


def sent_to_all(shard, axis):
    peers = lax.axis_size(axis)
    return lax.all_to_all(
        jnp.broadcast_to(shard[None], (peers, *shard.shape)), axis, 0, 0, tiled=True
    )


def gather_directly(shard, axis, dim):
    return in_order(sent_to_all(shard, axis), dim)


def in_blocks(shard, dim, peers):
    before, after = (shard.shape[:dim], shard.shape[dim + 1 :])
    return jnp.moveaxis(shard.reshape(*before, peers, -1, *after), dim, 0)


def sent_and_summed(shard, axis, dim):
    peers = lax.axis_size(axis)
    pieces = lax.all_to_all(in_blocks(shard, dim, peers), axis, 0, 0, tiled=True)
    return jnp.sum(pieces.astype(jnp.float32), axis=0)


def sum_at_owner(shard, axis, dim):
    peers = lax.axis_size(axis)
    pieces = lax.all_to_all(in_blocks(shard, dim, peers), axis, 0, 0, tiled=True)
    return jnp.sum(pieces, axis=0)


def shards(queries, labels, pages):
    pages_here, patch_count, width = pages.shape
    token_count = queries.shape[1]
    first_page = lax.axis_index(("dp", "inner")) * pages_here

    def block_terms(query_block, label_block, page_grads):
        rows_count = query_block.shape[0]
        flat_rows = query_block.reshape(rows_count * token_count, width)
        query_grad = jnp.zeros((rows_count * token_count, width), jnp.float32)
        updated = []
        for page_slot in range(pages_here):
            page_block = pages[page_slot]
            scores = lax.dot_general(
                flat_rows, page_block, (((1,), (1,)), ((), ())), preferred_element_type=jnp.float32
            )
            weights = jax.nn.softmax(scores, axis=-1)
            matched = jnp.sum(weights * scores, axis=-1)
            summed = matched.reshape(rows_count, token_count).sum(axis=1)
            signs = jnp.where(
                label_block == first_page + page_slot, jnp.float32(1.0), jnp.float32(-1.0)
            )
            logits = summed - jnp.float32(token_count)
            grad_score = -signs * jax.nn.sigmoid(-signs * logits)
            row_grad = jnp.broadcast_to(grad_score[:, None], (rows_count, token_count)).reshape(
                rows_count * token_count
            )
            dscore = (row_grad[:, None] * weights * (1.0 + scores - matched[:, None])).astype(
                jnp.bfloat16
            )
            query_grad = query_grad + jnp.dot(
                dscore, page_block, preferred_element_type=jnp.float32
            )
            page_term = lax.dot_general(
                dscore, flat_rows, (((0,), (0,)), ((), ())), preferred_element_type=jnp.float32
            )
            updated.append(page_grads[page_slot] + page_term)
        return (query_grad.reshape(rows_count, token_count, width), jnp.stack(updated))

    empty_pages = jnp.zeros((pages_here, patch_count, width), jnp.float32)
    nearby_rows = (gather_directly(queries, "inner", 0), gather_directly(labels, "inner", 0))
    page_grads = empty_pages
    query_piece = gather_directly(nearby_rows[0], "dp", 0)
    label_piece = gather_directly(nearby_rows[1], "dp", 0)
    accumulate_page_grads = page_grads
    rows_count = query_piece.shape[0]
    query_blocks = query_piece.reshape(rows_count // 16, 16, token_count, width)
    label_blocks = label_piece.reshape(rows_count // 16, 16)

    def advance(page_carry, inputs):
        block_grad, page_carry = block_terms(inputs[0], inputs[1], page_carry)
        return (page_carry, block_grad)

    accumulate_page_grads, block_grads = lax.scan(
        advance, accumulate_page_grads, (query_blocks, label_blocks)
    )
    piece_grad = block_grads.reshape(rows_count, token_count, width)
    page_grads = accumulate_page_grads
    grad_buffer = piece_grad
    grad_buffer, grad_pages = (grad_buffer, page_grads)
    partial_sum = sent_and_summed(grad_buffer.astype(jnp.bfloat16), "dp", 0)
    grad_queries = sum_at_owner(partial_sum, "inner", 0)
    return (grad_queries, grad_pages)


def solution(mesh):
    placed = (P(("dp", "inner"), None, None), P(("dp", "inner")), P(("dp", "inner"), None, None))
    return jax.shard_map(
        shards,
        mesh=mesh,
        in_specs=placed,
        out_specs=(P(("dp", "inner"), None, None), P(("dp", "inner"), None, None)),
        check_vma=False,
    )
```

profile of v0, /device:TPU:1, one launch (start us, length us, event | category | flops | bytes accessed | tf_op | source)
XLA Modules:
  0.0 366.6 jit_solution(4219806762628450248)
XLA Ops:
  1.9 9.1 %all-to-all-start = ((s32[16,1,1]{2,1,0:T(1,128)}), s32[16,1,1]{2,1,0:T(1,128)S(1)}, u32[]{:S(2)}, u32[]{:S(2)}) async-start(s32[16,1,1]{2,1,0:T(1,128)} %broadcast_in_dim.119), calls=%async_computation | async-start | bytes 16384 | tf_op jit(solution)/shard_map/all_to_all | solution.py:15
  11.0 6.9 %all-to-all-done = s32[16,1,1]{2,1,0:T(1,128)S(1)} async-done(((s32[16,1,1]{2,1,0:T(1,128)}), s32[16,1,1]{2,1,0:T(1,128)S(1)}, u32[]{:S(2)}, u32[]{:S(2)}) %all-to-all-start) | async-done | bytes 96 | tf_op jit(solution)/shard_map/all_to_all | solution.py:15
  18.3 9.5 %all_to_all.35 = s32[8,1,16]{2,1,0:T(1,128)S(1)} all-to-all(s32[8,1,16]{2,1,0:T(1,128)S(1)} %broadcast_in_dim.121), channel_id=1, replica_groups=mesh['dp'=8,'inner'=16] {'dp'}, dimensions={0} | all-to-all | bytes 1024 | tf_op jit(solution)/shard_map/all_to_all | solution.py:15
  28.5 12.5 %all_to_all.36 = bf16[16,1,32,128]{3,2,1,0:T(8,128)(2,1)S(1)} all-to-all(bf16[16,1,32,128]{3,2,1,0:T(8,128)(2,1)S(1)} %broadcast_in_dim.123), channel_id=1, replica_groups=mesh['dp'=8,'inner'=16] {'inner'}, dimensions={0} | all-to-all | bytes 262144 | tf_op jit(solution)/shard_map/all_to_all | solution.py:15
  42.2 3.7 %all-to-all-start.3 = ((bf16[8,16,32,128]{3,2,1,0:T(8,128)(2,1)}), bf16[8,16,32,128]{3,2,1,0:T(8,128)(2,1)S(1)}, u32[]{:S(2)}, u32[]{:S(2)}) async-start(bf16[8,16,32,128]{3,2,1,0:T(8,128)(2,1)} %broadcast_in_dim.125), calls=%async_computation.3 | async-start | bytes 2097152 | tf_op jit(solution)/shard_map/all_to_all | solution.py:15
  45.9 15.8 %all-to-all-done.3 = bf16[8,16,32,128]{3,2,1,0:T(8,128)(2,1)S(1)} async-done(((bf16[8,16,32,128]{3,2,1,0:T(8,128)(2,1)}), bf16[8,16,32,128]{3,2,1,0:T(8,128)(2,1)S(1)}, u32[]{:S(2)}, u32[]{:S(2)}) %all-to-all-start.3) | async-done | bytes 1048608 | tf_op jit(solution)/shard_map/all_to_all | solution.py:15
  63.2 271.4 %while.15 = (s32[]{:T(128)}, f32[4,1024,128]{2,1,0:T(8,128)}, bf16[8,16,32,128]{3,2,1,0:T(8,128)(2,1)}, s32[8,16]{1,0:T(8,128)S(1)}, s32[]{:T(128)}, /*index=5*/...) while((s32[]{:T(128)}, f32[4,1024,128]{2,1,0:T(8,128)}, ...), condition=%wide.region_17.18_spmd, body=%wide.region_0.17_spmd.sunk | while | flops 1642328576 | bytes 112491112 | solution.py:93
  74.8 2.3 fusion.125
  80.5 3.3 multiply_convert_fusion.8
  83.9 2.3 multiply_convert_fusion.9
  108.8 2.3 fusion.125
  114.4 3.3 multiply_convert_fusion.8
  117.8 2.3 multiply_convert_fusion.9
  142.7 2.3 fusion.125
  148.3 3.3 multiply_convert_fusion.8
  151.7 2.3 multiply_convert_fusion.9
  176.6 2.3 fusion.125
  182.2 3.3 multiply_convert_fusion.8
  185.6 2.3 multiply_convert_fusion.9
  210.5 2.3 fusion.125
  216.1 3.3 multiply_convert_fusion.8
  219.6 2.3 multiply_convert_fusion.9
  244.4 2.3 fusion.125
  250.1 3.3 multiply_convert_fusion.8
  253.5 2.3 multiply_convert_fusion.9
  278.4 2.3 fusion.125
  284.0 3.3 multiply_convert_fusion.8
  287.4 2.3 multiply_convert_fusion.9
  312.3 2.3 fusion.125
  317.9 3.3 multiply_convert_fusion.8
  334.5 18.3 %all_to_all.37 = bf16[8,16,32,128]{3,2,1,0:T(8,128)(2,1)S(1)} all-to-all(bf16[8,16,32,128]{3,2,1,0:T(8,128)(2,1)} %get-tuple-element.296), channel_id=1, replica_groups=mesh['dp'=8,'inner'=16] {'dp'}, dimensions={0} | all-to-all | bytes 2097152 | tf_op jit(solution)/shard_map/all_to_all | solution.py:31
  352.9 13.1 %all_to_all.38 = f32[16,1,32,128]{3,2,1,0:T(8,128)S(1)} all-to-all(f32[16,1,32,128]{3,2,1,0:T(8,128)S(1)} %bitcast.166), channel_id=1, replica_groups=mesh['dp'=8,'inner'=16] {'inner'}, dimensions={0} | all-to-all | bytes 524288 | tf_op jit(solution)/shard_map/all_to_all | solution.py:37
  (620 shorter events, 214.1 us)
Async XLA Ops:
  1.9 16.1 %all-to-all-start = ((s32[16,1,1]{2,1,0:T(1,128)}), s32[16,1,1]{2,1,0:T(1,128)S(1)}, u32[]{:S(2)}, u32[]{:S(2)}) async-start(s32[16,1,1]{2,1,0:T(1,128)} %broadcast_in_dim.119), calls=%async_computation | async-start | bytes 16384 | tf_op jit(solution)/shard_map/all_to_all | solution.py:15
  42.2 21.0 %copy-start.4 = (bf16[4,1024,128]{2,1,0:T(8,128)(2,1)S(1)}, bf16[4,1024,128]{2,1,0:T(8,128)(2,1)}, u32[]{:S(2)}) copy-start(bf16[4,1024,128]{2,1,0:T(8,128)(2,1)} %param.7) | copy-start | bytes 3145732
  42.2 19.5 %all-to-all-start.3 = ((bf16[8,16,32,128]{3,2,1,0:T(8,128)(2,1)}), bf16[8,16,32,128]{3,2,1,0:T(8,128)(2,1)S(1)}, u32[]{:S(2)}, u32[]{:S(2)}) async-start(bf16[8,16,32,128]{3,2,1,0:T(8,128)(2,1)} %broadcast_in_dim.125), calls=%async_computation.3 | async-start | bytes 2097152 | tf_op jit(solution)/shard_map/all_to_all | solution.py:15
  63.2 8.2 %copy-start.16 = (s32[8,16]{1,0:T(8,128)}, s32[8,16]{1,0:T(8,128)S(1)}, u32[]{:S(2)}) copy-start(s32[8,16]{1,0:T(8,128)S(1)} %get-tuple-element.285) | copy-start | bytes 1540 | tf_op jit(solution)/shard_map/while
  87.5 2.9 copy-start.6
  94.8 2.3 copy-start.9
  94.8 2.3 copy-start.17
  97.1 8.2 %copy-start.16 = (s32[8,16]{1,0:T(8,128)}, s32[8,16]{1,0:T(8,128)S(1)}, u32[]{:S(2)}) copy-start(s32[8,16]{1,0:T(8,128)S(1)} %get-tuple-element.285) | copy-start | bytes 1540 | tf_op jit(solution)/shard_map/while
  121.4 2.9 copy-start.6
  128.7 2.3 copy-start.9
  128.7 2.3 copy-start.17
  131.0 8.2 %copy-start.16 = (s32[8,16]{1,0:T(8,128)}, s32[8,16]{1,0:T(8,128)S(1)}, u32[]{:S(2)}) copy-start(s32[8,16]{1,0:T(8,128)S(1)} %get-tuple-element.285) | copy-start | bytes 1540 | tf_op jit(solution)/shard_map/while
  155.3 2.9 copy-start.6
  162.6 2.3 copy-start.9
  162.6 2.3 copy-start.17
  164.9 8.2 %copy-start.16 = (s32[8,16]{1,0:T(8,128)}, s32[8,16]{1,0:T(8,128)S(1)}, u32[]{:S(2)}) copy-start(s32[8,16]{1,0:T(8,128)S(1)} %get-tuple-element.285) | copy-start | bytes 1540 | tf_op jit(solution)/shard_map/while
  189.2 2.9 copy-start.6
  196.6 2.3 copy-start.9
  196.6 2.3 copy-start.17
  198.8 8.2 %copy-start.16 = (s32[8,16]{1,0:T(8,128)}, s32[8,16]{1,0:T(8,128)S(1)}, u32[]{:S(2)}) copy-start(s32[8,16]{1,0:T(8,128)S(1)} %get-tuple-element.285) | copy-start | bytes 1540 | tf_op jit(solution)/shard_map/while
  223.1 2.9 copy-start.6
  230.5 2.3 copy-start.9
  230.5 2.3 copy-start.17
  232.8 8.2 %copy-start.16 = (s32[8,16]{1,0:T(8,128)}, s32[8,16]{1,0:T(8,128)S(1)}, u32[]{:S(2)}) copy-start(s32[8,16]{1,0:T(8,128)S(1)} %get-tuple-element.285) | copy-start | bytes 1540 | tf_op jit(solution)/shard_map/while
  257.1 2.9 copy-start.6
  264.4 2.3 copy-start.9
  266.7 8.2 %copy-start.16 = (s32[8,16]{1,0:T(8,128)}, s32[8,16]{1,0:T(8,128)S(1)}, u32[]{:S(2)}) copy-start(s32[8,16]{1,0:T(8,128)S(1)} %get-tuple-element.285) | copy-start | bytes 1540 | tf_op jit(solution)/shard_map/while
  291.0 2.9 copy-start.6
  298.3 2.3 copy-start.9
  300.6 8.2 %copy-start.16 = (s32[8,16]{1,0:T(8,128)}, s32[8,16]{1,0:T(8,128)S(1)}, u32[]{:S(2)}) copy-start(s32[8,16]{1,0:T(8,128)S(1)} %get-tuple-element.285) | copy-start | bytes 1540 | tf_op jit(solution)/shard_map/while
  324.9 2.9 copy-start.6
  332.2 2.3 copy-start.9
  (107 other events, 180.5 us)
where the time goes:
time: 369 us; the launch traced here: 367 us
  other arithmetic  144 us (39%)
  matrix products  84.3 us (23%)
  blocking collectives  53.3 us (14%)
  local copies, waits for them, and re-layouts  45.8 us (12%)
  waiting for transfers between devices  22.7 us (6%)
  starting transfers between devices  12.8 us (3%)
    convert_element_type x32, other arithmetic, block_terms(): (row_grad[:, None] * weights * (1.0 + scores - matched[:, None])).astype(...  74.3 us
    dot_general x32, matrix products, block_terms(): jnp.dot(dscore, page_block, preferred_element_type=jnp.float32)  38.1 us
    dot_general x32, matrix products, block_terms(): lax.dot_general(dscore, flat_rows, (((0,), (0,)), ((), ())), preferred_el...  29.7 us
    all_to_all x2, waiting for transfers between devices, sent_to_all(): lax.all_to_all(jnp.broadcast_to(shard[None], (peers, *shard.shape)), axis...  22.7 us
    all_to_all x2, blocking collectives, sent_to_all(): lax.all_to_all(jnp.broadcast_to(shard[None], (peers, *shard.shape)), axis...  22 us
    while x272, local copies, waits for them, and re-layouts  19.9 us
    reduce_sum x32, other arithmetic, block_terms(): matched = jnp.sum(weights * scores, axis=-1)  18.9 us
    all_to_all x1, blocking collectives, sent_and_summed(): lax.all_to_all(in_blocks(shard, dim, peers), axis, 0, 0, tiled=True)  18.3 us
  transfers between devices with their start and end apart: 2, of which 2 were waited for; matrix products, arithmetic and copies ran while one was open for 0% of the time, Pallas kernels for 0%

commit v1 on v0

v1 whole, which is shorter than its diff:
```python
import functools

import jax
import jax.numpy as jnp
from jax import lax
from jax.experimental import pallas as pl
from jax.experimental.pallas import tpu as pltpu
from jax.sharding import PartitionSpec as P

LOG2E = 1.4426950408889634
LN2 = 0.6931471805599453
LQ = 32
RB = 512
TR = 32
HW = 256


def compute_kernel(lab_ref, q_ref, p_ref, first_ref, gp_ref, gq_ref, q2, p2, pt, s0, s1, m0, m1, e0, d0, d1, gacc):
    pages, lp, dd = p_ref.shape
    rows = q_ref.shape[0]
    rb = RB
    nblk = rows // rb
    first = first_ref[0]
    sbuf, mbuf, dbuf = (s0, s1), (m0, m1), (d0, d1)

    def split(i, _):
        at = pl.ds(pl.multiple_of(i * 256, 256), 256)
        x = q_ref[at, :].astype(jnp.float32) * LOG2E
        hi = x.astype(jnp.bfloat16)
        q2[at, :dd] = hi
        q2[at, dd:] = (x - hi.astype(jnp.float32)).astype(jnp.bfloat16)
        return 0
    lax.fori_loop(0, rows // 256, split, 0)
    for p in range(pages):
        for c in range(0, lp, 256):
            blk = p_ref[p, c:c + 256, :]
            p2[p, c:c + 256, :dd] = blk
            p2[p, c:c + 256, dd:] = blk
            pt[p, :, c:c + 256] = blk.T
    gp_ref[...] = jnp.zeros_like(gp_ref)
    gacc[...] = jnp.zeros_like(gacc)
    d1[...] = jnp.zeros_like(d1)

    def units_a(r, p, s_ref, m_ref):
        at = pl.ds(pl.multiple_of(r * rb, rb), rb)
        out = []
        state = {}

        def chunk(c):
            s = lax.dot_general(p2[p, c:c + 256, :], q2[at, :], (((1,), (1,)), ((), ())), preferred_element_type=jnp.float32)
            s_ref[c:c + 256, :] = s
            m = jnp.max(s.reshape(32, 8, rb), axis=0)
            state["m"] = m if c == 0 else jnp.maximum(state["m"], m)
            if c + 256 == lp:
                m_ref[...] = state["m"]
        return [functools.partial(chunk, c) for c in range(0, lp, 256)]

    def units_bc(r, p, s_ref, m_ref, d_ref):
        lane = lax.broadcasted_iota(jnp.int32, (8, 128), 1)
        st = {}
        b, c_ = [], []

        def start(h):
            m = m_ref[:, h:h + HW]
            m = jnp.broadcast_to(jnp.max(m, axis=0, keepdims=True), m.shape)
            st["m", h] = m
            st["l", h] = jnp.zeros((8, HW), jnp.float32)
            st["n", h] = jnp.zeros((8, HW), jnp.float32)

        def bt(h, k):
            if k == 0:
                start(h)
            y = s_ref[k:k + TR, h:h + HW].reshape(TR // 8, 8, HW)
            x = y - st["m", h][None]
            e = jnp.exp2(x)
            e0[k:k + TR, h:h + HW] = e.reshape(TR, HW)
            st["l", h] += jnp.sum(e, axis=0)
            st["n", h] += jnp.sum(e * x, axis=0)
            if k + TR == lp:
                finish(h)

        def finish(h):
            l = jnp.broadcast_to(jnp.sum(st["l", h], axis=0, keepdims=True), (8, HW))
            n = jnp.broadcast_to(jnp.sum(st["n", h], axis=0, keepdims=True), (8, HW))
            inv = 1.0 / l
            m2 = st["m", h] + n * inv
            tot = []
            for g in range(0, HW, 128):
                t = m2[:, g:g + 128]
                for w in (1, 2, 4, 8, 16):
                    up = pltpu.roll(t, 128 - w, 1)
                    dn = pltpu.roll(t, w, 1)
                    t = t + jnp.where((lane & w) == 0, up, dn)
                tot.append(t)
            score = jnp.concatenate(tot, axis=1) * LN2
            at = pl.ds(pl.multiple_of(r * rb + h, HW), HW)
            lab = lab_ref[:, at]
            sign = jnp.where(lab == first + p, 1.0, -1.0).astype(jnp.float32)
            g = -sign / (1.0 + jnp.exp(sign * (score - float(LQ))))
            st["a", h] = g * inv * LN2
            st["c", h] = m2 - LOG2E

        def ct(h, k):
            y = s_ref[k:k + TR, h:h + HW].reshape(TR // 8, 8, HW)
            e = e0[k:k + TR, h:h + HW].reshape(TR // 8, 8, HW)
            d = (e * st["a", h][None]) * (y - st["c", h][None])
            d_ref[k:k + TR, h:h + HW] = d.reshape(TR, HW).astype(jnp.bfloat16)

        us = []
        for h in range(0, rb, HW):
            us += [functools.partial(bt, h, k) for k in range(0, lp, TR)]
        for h in range(0, rb, HW):
            us += [functools.partial(ct, h, k) for k in range(0, lp, TR)]
        return us

    def units_d(r, p, d_ref):
        at = pl.ds(pl.multiple_of(r * rb, rb), rb)
        st = {}

        def gq(c):
            t = jnp.dot(pt[p, :, c:c + 256], d_ref[c:c + 256, :], preferred_element_type=jnp.float32)
            st["g"] = t if c == 0 else st["g"] + t
            if c + 256 == lp:
                if p == 0:
                    gacc[...] = st["g"]
                elif p < pages - 1:
                    gacc[...] += st["g"]
                else:
                    tot = gacc[...] + st["g"]
                    for k in range(0, rb, 128):
                        gq_ref[pl.ds(pl.multiple_of(r * rb + k, 128), 128), :] = tot[:, k:k + 128].T.astype(gq_ref.dtype)

        def gp(c):
            gp_ref[p, c:c + 256, :] += jnp.dot(d_ref[c:c + 256, :], q_ref[at, :], preferred_element_type=jnp.float32)

        us = []
        for c in range(0, lp, 256):
            us += [functools.partial(gq, c), functools.partial(gp, c)]
        return us

    def weave(vec, mxu):
        n, k = len(vec), len(mxu)
        j = 0
        for i, u in enumerate(vec):
            while j < k and j * n <= i * k:
                mxu[j]()
                j += 1
            u()
        while j < k:
            mxu[j]()
            j += 1

    for u in units_a(0, 0, s0, m0):
        u()

    def body(r, _):
        for p in range(pages):
            nr = r if p + 1 < pages else jnp.minimum(r + 1, nblk - 1)
            a = units_a(nr, (p + 1) % pages, sbuf[(p + 1) % 2], mbuf[(p + 1) % 2])
            bc = units_bc(r, p, sbuf[p % 2], mbuf[p % 2], dbuf[p % 2])
            d = units_d(r if p > 0 else jnp.maximum(r - 1, 0), (p - 1) % pages, dbuf[(p - 1) % 2])
            mx = []
            for i in range(4):
                mx += [d[2 * i], d[2 * i + 1], a[i]]
            weave(bc, mx)
        return 0

    lax.fori_loop(0, nblk, body, 0)
    for u in units_d(nblk - 1, pages - 1, dbuf[(pages - 1) % 2]):
        u()


def compute(lab, q, p, first):
    pages, lp, dd = p.shape
    rows = q.shape[0]
    vm = pl.BlockSpec(memory_space=pltpu.VMEM)
    return pl.pallas_call(
        compute_kernel,
        out_shape=(jax.ShapeDtypeStruct((pages, lp, dd), jnp.float32), jax.ShapeDtypeStruct((rows, dd), jnp.bfloat16)),
        in_specs=[vm, vm, vm, pl.BlockSpec(memory_space=pltpu.SMEM)],
        out_specs=(vm, vm),
        scratch_shapes=[
            pltpu.VMEM((rows, 2 * dd), jnp.bfloat16),
            pltpu.VMEM((pages, lp, 2 * dd), jnp.bfloat16),
            pltpu.VMEM((pages, dd, lp), jnp.bfloat16),
            pltpu.VMEM((lp, RB), jnp.float32), pltpu.VMEM((lp, RB), jnp.float32),
            pltpu.VMEM((8, RB), jnp.float32), pltpu.VMEM((8, RB), jnp.float32),
            pltpu.VMEM((lp, RB), jnp.float32),
            pltpu.VMEM((lp, RB), jnp.bfloat16), pltpu.VMEM((lp, RB), jnp.bfloat16),
            pltpu.VMEM((dd, RB), jnp.float32),
        ],
        compiler_params=pltpu.CompilerParams(vmem_limit_bytes=60 << 20),
        name="late_interaction",
    )(lab, q, p, first)


def in_order(pieces, dim):
    pieces = jnp.moveaxis(pieces, 0, dim)
    shape = pieces.shape
    return pieces.reshape(*shape[:dim], shape[dim] * shape[dim + 1], *shape[dim + 2 :])


def sent_to_all(shard, axis):
    peers = lax.axis_size(axis)
    return lax.all_to_all(
        jnp.broadcast_to(shard[None], (peers, *shard.shape)), axis, 0, 0, tiled=True
    )


def gather_directly(shard, axis, dim):
    return in_order(sent_to_all(shard, axis), dim)


def in_blocks(shard, dim, peers):
    before, after = (shard.shape[:dim], shard.shape[dim + 1 :])
    return jnp.moveaxis(shard.reshape(*before, peers, -1, *after), dim, 0)


def summed(shard, axis, dim):
    peers = lax.axis_size(axis)
    pieces = lax.all_to_all(in_blocks(shard, dim, peers), axis, 0, 0, tiled=True)
    return jnp.sum(pieces.astype(jnp.float32), axis=0)


def shards(queries, labels, pages):
    first = lax.axis_index(("dp", "inner")) * pages.shape[0]
    token_count, width = queries.shape[1:]
    rows = gather_directly(gather_directly(queries, "inner", 0), "dp", 0)
    labs = gather_directly(gather_directly(labels, "inner", 0), "dp", 0)
    count = rows.shape[0]
    flat = rows.reshape(count * token_count, width)
    lab8 = jnp.broadcast_to(jnp.repeat(labs, token_count)[None], (8, count * token_count))
    grad_pages, partial = compute(lab8, flat, pages, first.astype(jnp.int32).reshape(1))
    partial = partial.reshape(count, token_count, width)
    grad_queries = summed(summed(partial, "dp", 0), "inner", 0)
    return grad_queries, grad_pages


def solution(mesh):
    placed = (P(("dp", "inner"), None, None), P(("dp", "inner")), P(("dp", "inner"), None, None))
    return jax.shard_map(
        shards,
        mesh=mesh,
        in_specs=placed,
        out_specs=(P(("dp", "inner"), None, None), P(("dp", "inner"), None, None)),
        check_vma=False,
    )
```

time: 369 us -> 148 us (0.40)
  other arithmetic: 144 us -> 1.81 us
  matrix products: 84.3 us -> 0 us
  Pallas kernels: 0 us -> 53.9 us
  local copies, waits for them, and re-layouts: 45.8 us -> 3.66 us
  blocking collectives: 53.3 us -> 69.3 us
  starting transfers between devices: 12.8 us -> 3.56 us
  waiting for transfers between devices: 22.7 us -> 14.4 us
    dot_general x96 -> x0, matrix products: 84.3 us -> none  [the longest x32 38.1 us: block_terms(): jnp.dot(dscore, page_block, preferred_element_type=jnp.float32)]
    convert_element_type x32 -> x0, other arithmetic: 74.3 us -> none  [block_terms(): (row_grad[:, None] * weights * (1.0 + scores - matched[:, None])).astype(...]
    pallas_call x0 -> x1, Pallas kernels: none -> 53.9 us  [compute(): pl.pallas_call(compute_kernel, out_shape=(jax.ShapeDtypeStruct((pages, lp...]
    reduce_sum x98 -> x2, other arithmetic: 48.5 us -> 0.77 us  [summed(): return jnp.sum(pieces.astype(jnp.float32), axis=0)]
    while x272 -> x0, local copies, waits for them, and re-layouts: 19.9 us -> none
    all_to_all x2 -> x3, blocking collectives: 22 us -> 37.9 us  [sent_to_all(): lax.all_to_all(jnp.broadcast_to(shard[None], (peers, *shard.shape)), axis...]
    another operation x8 -> x0, other arithmetic: 12.4 us -> none  [block_terms(): jnp.stack(updated)]
    all_to_all x2 -> x1, starting transfers between devices: 12.8 us -> 3.56 us  [sent_to_all(): lax.all_to_all(jnp.broadcast_to(shard[None], (peers, *shard.shape)), axis...]
  transfers between devices with their start and end apart: 2 -> 1, of which waited for: 2 -> 1; matrix products, arithmetic and copies ran while one was open for 0% -> 1% of each run, Pallas kernels for 0% -> 0%
where the time goes in v1:
time: 148 us
  blocking collectives  69.3 us (47%)
  Pallas kernels  53.9 us (36%)
  waiting for transfers between devices  14.4 us (10%)
  local copies, waits for them, and re-layouts  3.66 us (2%)
  starting transfers between devices  3.56 us (2%)
  other arithmetic  1.81 us (1%)
    pallas_call x1, Pallas kernels, compute(): pl.pallas_call(compute_kernel, out_shape=(jax.ShapeDtypeStruct((pages, lp...  53.9 us
    all_to_all x3, blocking collectives, sent_to_all(): lax.all_to_all(jnp.broadcast_to(shard[None], (peers, *shard.shape)), axis...  37.9 us
    all_to_all x2, blocking collectives, summed(): lax.all_to_all(in_blocks(shard, dim, peers), axis, 0, 0, tiled=True)  31.3 us
    all_to_all x1, waiting for transfers between devices, sent_to_all(): lax.all_to_all(jnp.broadcast_to(shard[None], (peers, *shard.shape)), axis...  14.4 us
    all_to_all x1, starting transfers between devices, sent_to_all(): lax.all_to_all(jnp.broadcast_to(shard[None], (peers, *shard.shape)), axis...  3.56 us
  transfers between devices with their start and end apart: 1, of which 1 were waited for; matrix products, arithmetic and copies ran while one was open for 1% of the time, Pallas kernels for 0%

profile of v1, /device:TPU:1, one launch (start us, length us, event | category | flops | bytes accessed | tf_op | source)
XLA Modules:
  0.0 147.9 jit_solution(1441648353049270912)
XLA Ops:
  1.3 15.9 %all_to_all.32 = s32[16,1,1]{2,1,0:T(1,128)S(1)} all-to-all(s32[16,1,1]{2,1,0:T(1,128)S(1)} %broadcast_in_dim.41), channel_id=1, replica_groups=mesh['dp'=8,'inner'=16] {'inner'}, dimensions={0} | all-to-all | bytes 128 | tf_op jit(solution)/shard_map/all_to_all | solution.py:205
  17.2 0.4 reduce.1
  17.6 9.5 %all_to_all.33 = s32[8,1,16]{2,1,0:T(1,128)S(1)} all-to-all(s32[8,1,16]{2,1,0:T(1,128)S(1)} %broadcast_in_dim.43), channel_id=1, replica_groups=mesh['dp'=8,'inner'=16] {'dp'}, dimensions={0} | all-to-all | bytes 1024 | tf_op jit(solution)/shard_map/all_to_all | solution.py:205
  27.1 0.7 broadcast_in_dim.48
  27.8 12.5 %all_to_all.34 = bf16[16,1,32,128]{3,2,1,0:T(8,128)(2,1)S(1)} all-to-all(bf16[16,1,32,128]{3,2,1,0:T(8,128)(2,1)S(1)} %broadcast_in_dim.48), channel_id=1, replica_groups=mesh['dp'=8,'inner'=16] {'inner'}, dimensions={0} | all-to-all | bytes 262144 | tf_op jit(solution)/shard_map/all_to_all | solution.py:205
  40.3 1.1 broadcast_in_dim.50
  41.5 3.6 %all-to-all-start.3 = ((bf16[8,16,32,128]{3,2,1,0:T(8,128)(2,1)}), bf16[8,16,32,128]{3,2,1,0:T(8,128)(2,1)S(1)}, u32[]{:S(2)}, u32[]{:S(2)}) async-start(bf16[8,16,32,128]{3,2,1,0:T(8,128)(2,1)} %broadcast_in_dim.50), calls=%async_computation.3 | async-start | bytes 2097152 | tf_op jit(solution)/shard_map/all_to_all | solution.py:205
  45.0 0.5 broadcast.10
  45.6 0.7 reduce.5
  46.2 0.1 reshape.34
  46.3 0.1 broadcast_in_dim.44
  46.4 0.1 broadcast_in_dim.45
  46.5 14.4 %all-to-all-done.3 = bf16[8,16,32,128]{3,2,1,0:T(8,128)(2,1)S(1)} async-done(((bf16[8,16,32,128]{3,2,1,0:T(8,128)(2,1)}), bf16[8,16,32,128]{3,2,1,0:T(8,128)(2,1)S(1)}, u32[]{:S(2)}, u32[]{:S(2)}) %all-to-all-start.3) | async-done | bytes 1048608 | tf_op jit(solution)/shard_map/all_to_all | solution.py:205
  60.8 0.0 copy-start
  60.9 0.7 broadcast_in_dim.46.lab_ref
  61.5 0.3 copy-done
  61.9 53.9 %late_interaction.1 = (f32[4,1024,128]{2,1,0:T(8,128)}, bf16[4096,128]{1,0:T(8,128)(2,1)}) custom-call(s32[8,4096]{1,0:T(8,128)} %broadcast_in_dim.46.lab_ref, bf16[4096,128]{1,0:T(8,128)(2,1)} %bitcast.9, bf16[4,1024,128]{2,1,0:T(8,128)(2,1)} %p_ref.1, s32[1]{0:T(128)} %bitcast.4.first_ref), custom_call_target="tpu_custom_call" | custom-call | tf_op jit(solution)/shard_map/late_interaction/pallas_call | solution.py:177
  115.8 18.3 %all_to_all.35 = bf16[8,16,32,128]{3,2,1,0:T(8,128)(2,1)S(1)} all-to-all(bf16[8,16,32,128]{3,2,1,0:T(8,128)(2,1)} %bitcast.11), channel_id=1, replica_groups=mesh['dp'=8,'inner'=16] {'dp'}, dimensions={0} | all-to-all | bytes 2097152 | tf_op jit(solution)/shard_map/all_to_all | solution.py:221
  134.1 0.1 convert_reduce_fusion
  134.2 13.1 %all_to_all.36 = f32[16,1,32,128]{3,2,1,0:T(8,128)S(1)} all-to-all(f32[16,1,32,128]{3,2,1,0:T(8,128)S(1)} %bitcast.10), channel_id=1, replica_groups=mesh['dp'=8,'inner'=16] {'inner'}, dimensions={0} | all-to-all | bytes 524288 | tf_op jit(solution)/shard_map/all_to_all | solution.py:221
  147.3 0.6 reduce_sum.21
  (2 shorter events, 0.0 us)
Async XLA Ops:
  41.5 19.4 %all-to-all-start.3 = ((bf16[8,16,32,128]{3,2,1,0:T(8,128)(2,1)}), bf16[8,16,32,128]{3,2,1,0:T(8,128)(2,1)S(1)}, u32[]{:S(2)}, u32[]{:S(2)}) async-start(bf16[8,16,32,128]{3,2,1,0:T(8,128)(2,1)} %broadcast_in_dim.50), calls=%async_computation.3 | async-start | bytes 2097152 | tf_op jit(solution)/shard_map/all_to_all | solution.py:205
  60.8 1.0 copy-start

commit v2 on v1

v2 whole, which is shorter than its diff:
```python
import functools

import jax
import jax.numpy as jnp
from jax import lax
from jax.experimental import pallas as pl
from jax.experimental.pallas import tpu as pltpu
from jax.sharding import PartitionSpec as P

LOG2E = 1.4426950408889634
LN2 = 0.6931471805599453
LQ = 32
RB = 512
TR = 1024
HW = 256


MESH = pl.DeviceIdType.MESH


def step_kernel(lab_ref, q_ref, p_hbm, gp_ref, out_ref, p_ref, q_buf, l_buf, part, recv, q2, p2, pt, s0, s1, m0, m1, e0, d0, d1, gacc,
                p_sem, q_sem, l_sem, r_sem, qs_sem, ls_sem, rs_sem):
    pages, lp, dd = p_ref.shape
    ndp, nin = lax.axis_size("dp"), lax.axis_size("inner")
    dp, inner = lax.axis_index("dp"), lax.axis_index("inner")
    me = dp * nin + inner
    total = ndp * nin
    rb = RB
    nblk = ndp
    first = me * pages
    sbuf, mbuf, dbuf = (s0, s1), (m0, m1), (d0, d1)

    barrier = pltpu.get_barrier_semaphore()
    fetch = pltpu.make_async_copy(p_hbm, p_ref, p_sem)
    fetch.start()

    def greet(k, _):
        t = lax.rem(me + k, total)
        pl.semaphore_signal(barrier, inc=1, device_id={"dp": t // nin, "inner": lax.rem(t, nin)}, device_id_type=MESH)
        return 0
    lax.fori_loop(1, total, greet, 0)

    own = pl.ds(pl.multiple_of(me * LQ, LQ), LQ)
    q_buf[own, :] = q_ref[0]
    l_buf[pl.ds(me, 1), :, :] = jnp.full((1, 1, 128), lab_ref[0], jnp.int32)
    gp_ref[...] = jnp.zeros_like(gp_ref)
    gacc[...] = jnp.zeros_like(gacc)
    d1[...] = jnp.zeros_like(d1)
    fetch.wait()
    for p in range(pages):
        for c in range(0, lp, 256):
            blk = p_ref[p, c:c + 256, :]
            p2[p, c:c + 256, :dd] = blk
            p2[p, c:c + 256, dd:] = blk
            pt[p, :, c:c + 256] = blk.T
    pl.semaphore_wait(barrier, total - 1)

    def q_copy(t_dp, t_in):
        return pltpu.make_async_remote_copy(
            src_ref=q_buf.at[own, :], dst_ref=q_buf.at[own, :], send_sem=qs_sem, recv_sem=q_sem.at[dp],
            device_id={"dp": t_dp, "inner": t_in}, device_id_type=MESH)

    def l_copy(t_dp, t_in):
        return pltpu.make_async_remote_copy(
            src_ref=l_buf.at[me], dst_ref=l_buf.at[me], send_sem=ls_sem, recv_sem=l_sem.at[dp],
            device_id={"dp": t_dp, "inner": t_in}, device_id_type=MESH)

    def part_copy(r, t_in):
        rows = pl.ds(pl.multiple_of(r * rb + t_in * LQ, LQ), LQ)
        return pltpu.make_async_remote_copy(
            src_ref=part.at[rows, :], dst_ref=recv.at[me], send_sem=rs_sem, recv_sem=r_sem,
            device_id={"dp": r, "inner": t_in}, device_id_type=MESH)

    def share(k, _):
        t_dp, t_in = lax.rem(dp + ndp - k // nin, ndp), lax.rem(inner + k, nin)
        q_copy(t_dp, t_in).start()
        l_copy(t_dp, t_in).start()
        return 0
    lax.fori_loop(1, 2 * nin, share, 0)

    def block(k):
        return lax.rem(dp + k, ndp)

    def arrived(k, r, count):
        qs, ls = q_buf.at[pl.ds(0, count * LQ), :], l_buf.at[pl.ds(0, count)]
        pltpu.make_async_copy(qs, qs, q_sem.at[r]).wait()
        pltpu.make_async_copy(ls, ls, l_sem.at[r]).wait()

    def split(r):
        for c in range(0, rb, 256):
            at = pl.ds(pl.multiple_of(r * rb + c, 256), 256)
            x = q_buf[at, :].astype(jnp.float32) * LOG2E
            hi = x.astype(jnp.bfloat16)
            q2[at, :dd] = hi
            q2[at, dd:] = (x - hi.astype(jnp.float32)).astype(jnp.bfloat16)

    def send(k):
        r = block(k)

        def one(i, _):
            t_in = lax.rem(inner + i, nin)

            @pl.when(i + k > 0)
            def _():
                part_copy(r, t_in).start()
            return 0
        lax.fori_loop(0, nin, one, 0)

    def units_a(r, p, s_ref, m_ref):
        at = pl.ds(pl.multiple_of(r * rb, rb), rb)

        def scores():
            s = lax.dot_general(p2[p], q2[at, :], (((1,), (1,)), ((), ())), preferred_element_type=jnp.float32)
            s_ref[...] = s
            m_ref[...] = jnp.max(s.reshape(lp // 8, 8, rb), axis=0)
        return [scores]

    def units_bc(r, p, s_ref, m_ref, d_ref):
        lane = lax.broadcasted_iota(jnp.int32, (8, 128), 1)
        st = {}
        b, c_ = [], []

        def start(h):
            m = m_ref[:, h:h + HW]
            m = jnp.broadcast_to(jnp.max(m, axis=0, keepdims=True), m.shape)
            st["m", h] = m
            st["l", h] = jnp.zeros((8, HW), jnp.float32)
            st["n", h] = jnp.zeros((8, HW), jnp.float32)

        def bt(h, k):
            if k == 0:
                start(h)
            y = s_ref[k:k + TR, h:h + HW].reshape(TR // 8, 8, HW)
            x = y - st["m", h][None]
            e = jnp.exp2(x)
            e0[k:k + TR, h:h + HW] = e.reshape(TR, HW)
            st["l", h] += jnp.sum(e, axis=0)
            st["n", h] += jnp.sum(e * x, axis=0)
            if k + TR == lp:
                finish(h)

        def finish(h):
            l = jnp.broadcast_to(jnp.sum(st["l", h], axis=0, keepdims=True), (8, HW))
            n = jnp.broadcast_to(jnp.sum(st["n", h], axis=0, keepdims=True), (8, HW))
            inv = 1.0 / l
            m2 = st["m", h] + n * inv
            tot = []
            for g in range(0, HW, 128):
                t = m2[:, g:g + 128]
                for w in (1, 2, 4, 8, 16):
                    up = pltpu.roll(t, 128 - w, 1)
                    dn = pltpu.roll(t, w, 1)
                    t = t + jnp.where((lane & w) == 0, up, dn)
                tot.append(t)
            score = jnp.concatenate(tot, axis=1) * LN2
            lab = []
            for g in range(0, HW, 128):
                rows = [jnp.broadcast_to(l_buf[r * (rb // LQ) + (h + g) // LQ + j], (8, 128)) for j in range(128 // LQ)]
                row = rows[-1]
                for j in range(128 // LQ - 2, -1, -1):
                    row = jnp.where(lane < (j + 1) * LQ, rows[j], row)
                lab.append(row)
            lab = jnp.concatenate(lab, axis=1)
            sign = jnp.where(lab == first + p, 1.0, -1.0).astype(jnp.float32)
            g = -sign / (1.0 + jnp.exp(sign * (score - float(LQ))))
            st["a", h] = g * inv * LN2
            st["c", h] = m2 - LOG2E

        def ct(h, k):
            y = s_ref[k:k + TR, h:h + HW].reshape(TR // 8, 8, HW)
            e = e0[k:k + TR, h:h + HW].reshape(TR // 8, 8, HW)
            d = (e * st["a", h][None]) * (y - st["c", h][None])
            d_ref[k:k + TR, h:h + HW] = d.reshape(TR, HW).astype(jnp.bfloat16)

        us = []
        for h in range(0, rb, HW):
            us += [functools.partial(bt, h, k) for k in range(0, lp, TR)]
        for h in range(0, rb, HW):
            us += [functools.partial(ct, h, k) for k in range(0, lp, TR)]
        return us

    def units_d(r, p, d_ref):
        at = pl.ds(pl.multiple_of(r * rb, rb), rb)

        def gq():
            t = jnp.dot(pt[p], d_ref[...], preferred_element_type=jnp.float32)
            if p == 0:
                gacc[...] = t
            elif p < pages - 1:
                gacc[...] += t
            else:
                part[at, :] = (gacc[...] + t).T.astype(part.dtype)

        def gp():
            gp_ref[p] += jnp.dot(d_ref[...], q_buf[at, :], preferred_element_type=jnp.float32)

        return [gq, gp]

    def weave(vec, mxu):
        n, k = len(vec), len(mxu)
        j = 0
        for i, u in enumerate(vec):
            while j < k and j * n <= i * k:
                mxu[j]()
                j += 1
            u()
        while j < k:
            mxu[j]()
            j += 1

    arrived(0, dp, nin - 1)
    split(dp)
    for u in units_a(dp, 0, s0, m0):
        u()

    def body(k, _):
        r = block(k)
        nxt = block(jnp.minimum(k + 1, nblk - 1))
        prev = block(jnp.maximum(k - 1, 0))

        @pl.when(k + 1 < nblk)
        def _():
            arrived(k + 1, nxt, nin)

        @pl.when(k + 2 < nblk)
        def _():
            lax.fori_loop((k + 2) * nin, (k + 3) * nin, share, 0)
        split(nxt)
        for p in range(pages):
            nr = r if p + 1 < pages else nxt
            a = units_a(nr, (p + 1) % pages, sbuf[(p + 1) % 2], mbuf[(p + 1) % 2])
            bc = units_bc(r, p, sbuf[p % 2], mbuf[p % 2], dbuf[p % 2])
            d = units_d(r if p > 0 else prev, (p - 1) % pages, dbuf[(p - 1) % 2])
            weave(bc, d + a)

        @pl.when(k > 0)
        def _():
            send(k - 1)
        return 0

    lax.fori_loop(0, nblk, body, 0)
    last = block(nblk - 1)
    for u in units_d(last, pages - 1, dbuf[(pages - 1) % 2]):
        u()
    recv[pl.ds(me, 1), :, :] = part[own, :][None]
    send(nblk - 1)

    others = recv.at[pl.ds(0, total - 1)]
    pltpu.make_async_copy(others, others, r_sem).wait()

    def add(i, acc):
        blk = recv[pl.ds(pl.multiple_of(i * 8, 8), 8), :, :].astype(jnp.float32)
        return acc + jnp.sum(blk, axis=0)
    out_ref[0] = lax.fori_loop(0, total // 8, add, jnp.zeros((LQ, dd), jnp.float32))

    pltpu.make_async_copy(others, others, rs_sem).wait()
    pltpu.make_async_copy(others, others, qs_sem).wait()
    labels = l_buf.at[pl.ds(0, total - 1)]
    pltpu.make_async_copy(labels, labels, ls_sem).wait()


def shards(queries, labels, pages):
    count, lp, dd = pages.shape
    total = lax.axis_size("dp") * lax.axis_size("inner")
    rows = total * LQ
    vm = pl.BlockSpec(memory_space=pltpu.VMEM)
    f32, bf16 = jnp.float32, jnp.bfloat16
    grad_pages, grad_queries = pl.pallas_call(
        step_kernel,
        out_shape=(jax.ShapeDtypeStruct(pages.shape, f32), jax.ShapeDtypeStruct(queries.shape, f32)),
        in_specs=[pl.BlockSpec(memory_space=pltpu.SMEM), vm, pl.BlockSpec(memory_space=pl.ANY)],
        out_specs=(vm, vm),
        scratch_shapes=[
            pltpu.VMEM((count, lp, dd), bf16),
            pltpu.VMEM((rows, dd), bf16),
            pltpu.VMEM((total, 1, 128), jnp.int32),
            pltpu.VMEM((rows, dd), bf16),
            pltpu.VMEM((total, LQ, dd), bf16),
            pltpu.VMEM((rows, 2 * dd), bf16),
            pltpu.VMEM((count, lp, 2 * dd), bf16),
            pltpu.VMEM((count, dd, lp), bf16),
            pltpu.VMEM((lp, RB), f32), pltpu.VMEM((lp, RB), f32),
            pltpu.VMEM((8, RB), f32), pltpu.VMEM((8, RB), f32),
            pltpu.VMEM((lp, RB), f32),
            pltpu.VMEM((lp, RB), bf16), pltpu.VMEM((lp, RB), bf16),
            pltpu.VMEM((dd, RB), f32),
            pltpu.SemaphoreType.DMA,
            pltpu.SemaphoreType.DMA((8,)),
            pltpu.SemaphoreType.DMA((8,)),
            pltpu.SemaphoreType.DMA,
            pltpu.SemaphoreType.DMA,
            pltpu.SemaphoreType.DMA,
            pltpu.SemaphoreType.DMA,
        ],
        compiler_params=pltpu.CompilerParams(vmem_limit_bytes=36 << 20, collective_id=0, has_side_effects=True),
        name="late_interaction",
    )(labels, queries, pages)
    return grad_queries, grad_pages


def solution(mesh):
    placed = (P(("dp", "inner"), None, None), P(("dp", "inner")), P(("dp", "inner"), None, None))
    return jax.shard_map(
        shards,
        mesh=mesh,
        in_specs=placed,
        out_specs=(P(("dp", "inner"), None, None), P(("dp", "inner"), None, None)),
        check_vma=False,
    )
```

time: 148 us -> 87.9 us (0.59)
  blocking collectives: 69.3 us -> 0 us
  Pallas kernels: 53.9 us -> 82.5 us
  waiting for transfers between devices: 14.4 us -> 0 us
  starting transfers between devices: 3.56 us -> 0 us
  other arithmetic: 1.81 us -> 0 us
    all_to_all x5 -> x0, blocking collectives: 69.3 us -> none  [the longest x3 37.9 us: sent_to_all(): lax.all_to_all(jnp.broadcast_to(shard[None], (peers, *shard.shape)), axis...]
    pallas_call x1, Pallas kernels: 53.9 us -> 82.5 us  [shards(): pl.pallas_call(step_kernel, out_shape=(jax.ShapeDtypeStruct(pages.shape,...]
    all_to_all x1 -> x0, waiting for transfers between devices: 14.4 us -> none  [sent_to_all(): lax.all_to_all(jnp.broadcast_to(shard[None], (peers, *shard.shape)), axis...]
    all_to_all x1 -> x0, starting transfers between devices: 3.56 us -> none  [sent_to_all(): lax.all_to_all(jnp.broadcast_to(shard[None], (peers, *shard.shape)), axis...]
    unnamed x2 -> x6, local copies, waits for them, and re-layouts: 0.34 us -> 3.84 us
    broadcast_in_dim x7 -> x0, local copies, waits for them, and re-layouts: 2.73 us -> none  [the longest x4 1.88 us: sent_to_all(): jnp.broadcast_to(shard[None], (peers, *shard.shape))]
  transfers between devices with their start and end apart: 1 -> 0, of which waited for: 1 -> 0; matrix products, arithmetic and copies ran while one was open for 1% -> 0% of each run, Pallas kernels for 0% -> 0%
where the time goes in v2:
time: 87.9 us; the launch traced here: 87.7 us
  Pallas kernels  82.5 us (94%)
  local copies, waits for them, and re-layouts  3.84 us (4%)
  between operations  1.29 us (1%)
    pallas_call x1, Pallas kernels, shards(): pl.pallas_call(step_kernel, out_shape=(jax.ShapeDtypeStruct(pages.shape,...  82.5 us
    unnamed x6, local copies, waits for them, and re-layouts  3.84 us

profile of v2, /device:TPU:1, one launch (start us, length us, event | category | flops | bytes accessed | tf_op | source)
XLA Modules:
  0.0 87.7 jit_solution(13947873851864240326)
XLA Ops:
  1.3 0.0 copy-start
  1.3 1.2 %copy-done = bf16[4,1024,128]{2,1,0:T(8,128)(2,1)S(1)} copy-done((bf16[4,1024,128]{2,1,0:T(8,128)(2,1)S(1)}, bf16[4,1024,128]{2,1,0:T(8,128)(2,1)}, u32[]{:S(2)}) %copy-start) | copy-done | bytes 1048600
  2.5 0.0 copy-start.1
  2.5 0.7 copy-done.1
  3.2 82.5 %late_interaction.1 = (f32[4,1024,128]{2,1,0:T(8,128)S(1)}, f32[1,32,128]{2,1,0:T(8,128)S(1)}) custom-call(s32[1]{0:T(128)S(6)} %copy.7.lab_ref, bf16[1,32,128]{2,1,0:T(8,128)(2,1)S(1)} %copy-done.1, bf16[4,1024,128]{2,1,0:T(8,128)(2,1)S(1)} %copy-done), custom_call_target="tpu_custom_call" | custom-call | tf_op jit(solution)/shard_map/late_interaction/pallas_call | solution.py:268
  85.7 0.6 copy.8
  86.3 1.3 %copy.9 = f32[4,1024,128]{2,1,0:T(8,128)} copy(f32[4,1024,128]{2,1,0:T(8,128)S(1)} %get-tuple-element.9) | data formatting | bytes 4194304
Async XLA Ops:
  1.3 1.2 %copy-start = (bf16[4,1024,128]{2,1,0:T(8,128)(2,1)S(1)}, bf16[4,1024,128]{2,1,0:T(8,128)(2,1)}, u32[]{:S(2)}) copy-start(bf16[4,1024,128]{2,1,0:T(8,128)(2,1)} %p_hbm.1) | copy-start | bytes 3145732
  2.5 0.7 copy-start.1

commit v3 on v2

--- a/solution.py
+++ b/solution.py
@@ -11,8 +11,8 @@
 LN2 = 0.6931471805599453
 LQ = 32
 RB = 512
-TR = 1024
-HW = 256
+TR = 256
+HW = 512
 
 
 MESH = pl.DeviceIdType.MESH
@@ -34,49 +34,63 @@
     fetch = pltpu.make_async_copy(p_hbm, p_ref, p_sem)
     fetch.start()
 
-    def greet(k, _):
-        t = lax.rem(me + k, total)
-        pl.semaphore_signal(barrier, inc=1, device_id={"dp": t // nin, "inner": lax.rem(t, nin)}, device_id_type=MESH)
-        return 0
-    lax.fori_loop(1, total, greet, 0)
-
     own = pl.ds(pl.multiple_of(me * LQ, LQ), LQ)
     q_buf[own, :] = q_ref[0]
     l_buf[pl.ds(me, 1), :, :] = jnp.full((1, 1, 128), lab_ref[0], jnp.int32)
+
+    def greet(t_dp, t_in):
+        pl.semaphore_signal(barrier, inc=1, device_id={"dp": t_dp, "inner": t_in}, device_id_type=MESH)
+
+    dps = [lax.rem(dp + a, ndp) for a in range(8)]
+
+    def greet_all(b, _):
+        t_in = lax.rem(inner + b, nin)
+        for t_dp in dps:
+            greet(t_dp, t_in)
+        return 0
+    lax.fori_loop(1, nin, greet_all, 0)
+    for t_dp in dps[1:]:
+        greet(t_dp, inner)
+    pl.semaphore_wait(barrier, total - 1)
+
+    def q_copy(t_dp, t_in):
+        return pltpu.make_async_remote_copy(
+            src_ref=q_buf.at[own, :], dst_ref=q_buf.at[own, :], send_sem=qs_sem, recv_sem=q_sem.at[dp],
+            device_id={"dp": t_dp, "inner": t_in}, device_id_type=MESH)
+
+    def l_copy(t_dp, t_in):
+        return pltpu.make_async_remote_copy(
+            src_ref=l_buf.at[me], dst_ref=l_buf.at[me], send_sem=ls_sem, recv_sem=l_sem.at[dp],
+            device_id={"dp": t_dp, "inner": t_in}, device_id_type=MESH)
+
+    def part_copy(r, t_in):
+        rows = pl.ds(pl.multiple_of(r * rb + t_in * LQ, LQ), LQ)
+        return pltpu.make_async_remote_copy(
+            src_ref=part.at[rows, :], dst_ref=recv.at[me], send_sem=rs_sem, recv_sem=r_sem.at[dp],
+            device_id={"dp": r, "inner": t_in}, device_id_type=MESH)
+
+    def share(k, start):
+        t_dp = lax.rem(dp + ndp - k, ndp)
+
+        def one(i, _):
+            t_in = lax.rem(inner + i, nin)
+            q_copy(t_dp, t_in).start()
+            l_copy(t_dp, t_in).start()
+            return 0
+        lax.fori_loop(start, nin, one, 0)
+    share(0, 1)
+    share(1, 0)
+
     gp_ref[...] = jnp.zeros_like(gp_ref)
     gacc[...] = jnp.zeros_like(gacc)
     d1[...] = jnp.zeros_like(d1)
     fetch.wait()
     for p in range(pages):
-        for c in range(0, lp, 256):
-            blk = p_ref[p, c:c + 256, :]
-            p2[p, c:c + 256, :dd] = blk
-            p2[p, c:c + 256, dd:] = blk
-            pt[p, :, c:c + 256] = blk.T
-    pl.semaphore_wait(barrier, total - 1)
-
-    def q_copy(t_dp, t_in):
-        return pltpu.make_async_remote_copy(
-            src_ref=q_buf.at[own, :], dst_ref=q_buf.at[own, :], send_sem=qs_sem, recv_sem=q_sem.at[dp],
-            device_id={"dp": t_dp, "inner": t_in}, device_id_type=MESH)
-
-    def l_copy(t_dp, t_in):
-        return pltpu.make_async_remote_copy(
-            src_ref=l_buf.at[me], dst_ref=l_buf.at[me], send_sem=ls_sem, recv_sem=l_sem.at[dp],
-            device_id={"dp": t_dp, "inner": t_in}, device_id_type=MESH)
-
-    def part_copy(r, t_in):
-        rows = pl.ds(pl.multiple_of(r * rb + t_in * LQ, LQ), LQ)
-        return pltpu.make_async_remote_copy(
-            src_ref=part.at[rows, :], dst_ref=recv.at[me], send_sem=rs_sem, recv_sem=r_sem,
-            device_id={"dp": r, "inner": t_in}, device_id_type=MESH)
-
-    def share(k, _):
-        t_dp, t_in = lax.rem(dp + ndp - k // nin, ndp), lax.rem(inner + k, nin)
-        q_copy(t_dp, t_in).start()
-        l_copy(t_dp, t_in).start()
-        return 0
-    lax.fori_loop(1, 2 * nin, share, 0)
+        p2[p, :, :dd] = p_ref[p]
+        p2[p, :, dd:] = p_ref[p]
+        pt[p] = p_ref[p].T
+    share(2, 0)
+    share(3, 0)
 
     def block(k):
         return lax.rem(dp + k, ndp)
@@ -222,9 +236,9 @@
         def _():
             arrived(k + 1, nxt, nin)
 
-        @pl.when(k + 2 < nblk)
+        @pl.when(k + 4 < nblk)
         def _():
-            lax.fori_loop((k + 2) * nin, (k + 3) * nin, share, 0)
+            share(k + 4, 0)
         split(nxt)
         for p in range(pages):
             nr = r if p + 1 < pages else nxt
@@ -240,19 +254,30 @@
 
     lax.fori_loop(0, nblk, body, 0)
     last = block(nblk - 1)
-    for u in units_d(last, pages - 1, dbuf[(pages - 1) % 2]):
-        u()
+    grad_q, grad_p = units_d(last, pages - 1, dbuf[(pages - 1) % 2])
+    grad_q()
     recv[pl.ds(me, 1), :, :] = part[own, :][None]
     send(nblk - 1)
+    grad_p()
+
+    def landed(g, count):
+        got = recv.at[pl.ds(0, count)]
+        pltpu.make_async_copy(got, got, r_sem.at[g]).wait()
+
+    def summed(g):
+        terms = recv[pl.ds(pl.multiple_of(g * 16, 16), 16), :, :]
+        return jnp.sum(terms.astype(jnp.float32), axis=0)
+
+    landed(dp, nin - 1)
+    for a in range(2, 8):
+        landed(dps[a], nin)
+    tot = summed(dp)
+    for a in range(2, 8):
+        tot += summed(dps[a])
+    landed(dps[1], nin)
+    out_ref[0] = tot + summed(dps[1])
 
     others = recv.at[pl.ds(0, total - 1)]
-    pltpu.make_async_copy(others, others, r_sem).wait()
-
-    def add(i, acc):
-        blk = recv[pl.ds(pl.multiple_of(i * 8, 8), 8), :, :].astype(jnp.float32)
-        return acc + jnp.sum(blk, axis=0)
-    out_ref[0] = lax.fori_loop(0, total // 8, add, jnp.zeros((LQ, dd), jnp.float32))
-
     pltpu.make_async_copy(others, others, rs_sem).wait()
     pltpu.make_async_copy(others, others, qs_sem).wait()
     labels = l_buf.at[pl.ds(0, total - 1)]
@@ -287,7 +312,7 @@
             pltpu.SemaphoreType.DMA,
             pltpu.SemaphoreType.DMA((8,)),
             pltpu.SemaphoreType.DMA((8,)),
-            pltpu.SemaphoreType.DMA,
+            pltpu.SemaphoreType.DMA((8,)),
             pltpu.SemaphoreType.DMA,
             pltpu.SemaphoreType.DMA,
             pltpu.SemaphoreType.DMA,

time: 87.9 us -> 79.2 us (0.901)
  Pallas kernels: 82.5 us -> 73.9 us
    pallas_call x1, Pallas kernels: 82.5 us -> 73.9 us  [shards(): pl.pallas_call(step_kernel, out_shape=(jax.ShapeDtypeStruct(pages.shape,...]
where the time goes in v3:
time: 79.2 us; the launch traced here: 79 us
  Pallas kernels  73.9 us (93%)
  local copies, waits for them, and re-layouts  3.84 us (5%)
  between operations  1.29 us (2%)
    pallas_call x1, Pallas kernels, shards(): pl.pallas_call(step_kernel, out_shape=(jax.ShapeDtypeStruct(pages.shape,...  73.9 us
    unnamed x6, local copies, waits for them, and re-layouts  3.84 us

profile of v3, /device:TPU:1, one launch (start us, length us, event | category | flops | bytes accessed | tf_op | source)
XLA Modules:
  0.0 79.0 jit_solution(17271209897959714092)
XLA Ops:
  1.3 0.0 copy-start
  1.3 1.2 %copy-done = bf16[4,1024,128]{2,1,0:T(8,128)(2,1)S(1)} copy-done((bf16[4,1024,128]{2,1,0:T(8,128)(2,1)S(1)}, bf16[4,1024,128]{2,1,0:T(8,128)(2,1)}, u32[]{:S(2)}) %copy-start) | copy-done | bytes 1048600
  2.5 0.0 copy-start.1
  2.5 0.7 copy-done.1
  3.2 73.9 %late_interaction.1 = (f32[4,1024,128]{2,1,0:T(8,128)S(1)}, f32[1,32,128]{2,1,0:T(8,128)S(1)}) custom-call(s32[1]{0:T(128)S(6)} %copy.7.lab_ref, bf16[1,32,128]{2,1,0:T(8,128)(2,1)S(1)} %copy-done.1, bf16[4,1024,128]{2,1,0:T(8,128)(2,1)S(1)} %copy-done), custom_call_target="tpu_custom_call" | custom-call | tf_op jit(solution)/shard_map/late_interaction/pallas_call | solution.py:293
  77.1 0.6 copy.8
  77.7 1.3 %copy.9 = f32[4,1024,128]{2,1,0:T(8,128)} copy(f32[4,1024,128]{2,1,0:T(8,128)S(1)} %get-tuple-element.9) | data formatting | bytes 4194304
Async XLA Ops:
  1.3 1.2 %copy-start = (bf16[4,1024,128]{2,1,0:T(8,128)(2,1)S(1)}, bf16[4,1024,128]{2,1,0:T(8,128)(2,1)}, u32[]{:S(2)}) copy-start(bf16[4,1024,128]{2,1,0:T(8,128)(2,1)} %p_hbm.1) | copy-start | bytes 3145732
  2.5 0.7 copy-start.1

commit v4 on v3

--- a/solution.py
+++ b/solution.py
@@ -11,7 +11,7 @@
 LN2 = 0.6931471805599453
 LQ = 32
 RB = 512
-TR = 256
+TR = 128
 HW = 512
 
 

time: 79.2 us -> 78.7 us (level)
  no operation moved by 1% of the time
where the time goes in v4:
time: 78.7 us; the launch traced here: 78.5 us
  Pallas kernels  73.4 us (93%)
  local copies, waits for them, and re-layouts  3.84 us (5%)
  between operations  1.29 us (2%)
    pallas_call x1, Pallas kernels, shards(): pl.pallas_call(step_kernel, out_shape=(jax.ShapeDtypeStruct(pages.shape,...  73.4 us
    unnamed x6, local copies, waits for them, and re-layouts  3.84 us

profile of v4, /device:TPU:1, one launch (start us, length us, event | category | flops | bytes accessed | tf_op | source)
XLA Modules:
  0.0 78.5 jit_solution(18283034087144124768)
XLA Ops:
  1.3 0.0 copy-start
  1.3 1.2 %copy-done = bf16[4,1024,128]{2,1,0:T(8,128)(2,1)S(1)} copy-done((bf16[4,1024,128]{2,1,0:T(8,128)(2,1)S(1)}, bf16[4,1024,128]{2,1,0:T(8,128)(2,1)}, u32[]{:S(2)}) %copy-start) | copy-done | bytes 1048600
  2.5 0.0 copy-start.1
  2.5 0.7 copy-done.1
  3.2 73.4 %late_interaction.1 = (f32[4,1024,128]{2,1,0:T(8,128)S(1)}, f32[1,32,128]{2,1,0:T(8,128)S(1)}) custom-call(s32[1]{0:T(128)S(6)} %copy.7.lab_ref, bf16[1,32,128]{2,1,0:T(8,128)(2,1)S(1)} %copy-done.1, bf16[4,1024,128]{2,1,0:T(8,128)(2,1)S(1)} %copy-done), custom_call_target="tpu_custom_call" | custom-call | tf_op jit(solution)/shard_map/late_interaction/pallas_call | solution.py:293
  76.6 0.6 copy.8
  77.2 1.3 %copy.9 = f32[4,1024,128]{2,1,0:T(8,128)} copy(f32[4,1024,128]{2,1,0:T(8,128)S(1)} %get-tuple-element.9) | data formatting | bytes 4194304
Async XLA Ops:
  1.3 1.2 %copy-start = (bf16[4,1024,128]{2,1,0:T(8,128)(2,1)S(1)}, bf16[4,1024,128]{2,1,0:T(8,128)(2,1)}, u32[]{:S(2)}) copy-start(bf16[4,1024,128]{2,1,0:T(8,128)(2,1)} %p_hbm.1) | copy-start | bytes 3145732
  2.5 0.7 copy-start.1
